TPU v7x, 32 devices: a whole 2x2x4 slice. The times are simulated.
32 devices in a mesh: ta: 4 (over y, x), sa: 8 (over z, core).
Axes of the slice: x: 2, y: 2, z: 4, core: 2. Of those that a mesh axis runs over, the one named last changes fastest.
Arguments:
- eigvecs: float32 [2, 8, 64, 3, 4096], P(None, 'ta', None, None, 'sa'), may hold values from -0.0546875 to 0.0546875
- solutions: float32 [2, 8, 3, 8, 4, 3, 4096], P(None, 'ta', None, None, None, None, 'sa'), may hold values from -15 to 15
- source_times: int32 [3], replicated, may hold values from 0 to 7, as said below
- spin_dilution: int32 [3, 8], replicated, may hold values from 0 to 3
Outputs:
- perambulator: float32 [2, 8, 6144], P(None, 'ta', 'sa')
- norms: float32 [3, 8], replicated
Inputs may be any that keep to these rules, and one draw needn't show every extreme that they name: `source_times`: some source lies at slice 0 and another at slice 8 - 1.
All inputs are finite; a program needn't handle non-finite values.
Results may differ from a plain program's by a relative error of at most 0.000084.
Values sent between devices are 32-bit elements; how exact they have to be, the bound alone decides.
No kernel may reach another device: no remote copies, remote signals or barrier semaphores. Data moves between devices by JAX's collectives and lax.ppermute only.
A program may use at most 64 MiB of HBM per device.

v0:
```python
import functools

import jax
import jax.numpy as jnp
from jax import lax
from jax.experimental import pallas as pl
from jax.experimental.pallas import tpu as pltpu
from jax.sharding import PartitionSpec as P


F32 = jnp.float32
BF16 = jnp.bfloat16
SPINS = 4
COLORS = 3
LANES = 128
NT_DIMS = (((1,), (1,)), ((), ()))
VMEM_BYTES = 32 * 2**20
MASKS = (1, 3, 5)


def halves(x):
    high = x.astype(BF16)
    return high, (x - high.astype(F32)).astype(BF16)


def dot_nt(a, b, precision=None):
    return lax.dot_general(a, b, NT_DIMS, precision=precision, preferred_element_type=F32)


def split_kernel(s_hbm, split_ref, sums_ref, s_v, sems):
    _, times, pairs, rows, _ = s_hbm.shape
    columns = SPINS * pairs
    pitch = s_v.shape[3]
    chunk = rows // COLORS
    copies = []
    for t in range(times):
        for part in range(2):
            for color in range(COLORS):
                here = pl.ds(color * chunk, chunk)
                copy = pltpu.make_async_copy(
                    s_hbm.at[part, t, :, here],
                    s_v.at[part, t, :, here],
                    sems.at[part, t, color],
                )
                copy.start()
                copies.append((t, part, color, copy))
    squares = [jnp.zeros((pairs, LANES), F32) for _ in range(SPINS)]
    for t, part, color, copy in copies:
        copy.wait()
        flat = s_v.at[part, t].reshape(pairs * pitch, LANES)
        for block in range(color * chunk // SPINS, (color + 1) * chunk // SPINS):
            spins = [
                flat[pl.ds(block * SPINS + spin, pairs, stride=pitch), :]
                for spin in range(SPINS)
            ]
            for spin in range(SPINS):
                squares[spin] = squares[spin] + spins[spin] * spins[spin]
            high, low = halves(jnp.concatenate(spins, 0))
            split_ref[t, block, part * columns : (part + 1) * columns] = high
            split_ref[t, block, (2 + part) * columns : (3 + part) * columns] = low
    sums_ref[...] = (squares[0] + squares[1]) + (squares[2] + squares[3])


def row_kernel(sums_ref, row_ref, *, columns):
    pairs = sums_ref.shape[0]
    placed = jnp.concatenate(
        [
            jnp.zeros((columns, LANES), F32),
            sums_ref[...],
            jnp.zeros((LANES - columns - pairs, LANES), F32),
        ],
        0,
    )
    high, low = halves(placed)
    total = dot_nt(jnp.ones((16, 2 * LANES), BF16), jnp.concatenate([high, low], 1))
    row_ref[...] = total[:8]


def tile_kernel(split_ref, e_ref, *refs, masks):
    _, times, _, eigs, _ = e_ref.shape
    columns = split_ref.shape[2] // 4
    blocks = split_ref.shape[1]
    tiles = refs[-1]
    lane = lax.broadcasted_iota(jnp.int32, (columns, LANES), 1)
    for t in range(times):
        wide = []
        for color in range(COLORS):
            stack = jnp.concatenate([e_ref[0, t, color], e_ref[1, t, color]], 0)
            wide.append(jnp.concatenate(halves(stack), 0))
        left = jnp.concatenate([split_ref[t, block] for block in range(blocks)], 1)
        product = dot_nt(left, jnp.concatenate(wide, 1))
        top = product[: 2 * columns]
        joint = top[:, : 2 * eigs] + top[:, 2 * eigs :] + product[2 * columns :, : 2 * eigs]
        joint = joint + product[2 * columns :, 2 * eigs :]
        real = joint[:columns]
        imag = pltpu.roll(joint[columns:], eigs, 1)
        both = imag + jnp.where(lane < eigs, real, -real)
        both = jnp.concatenate([both, jnp.zeros((LANES - columns, LANES), F32)], 0).T
        both = both.reshape(2, eigs // 8, 8, LANES)
        tiles[:, t] = both[0]
        tiles[:, times + t] = both[1]
    if masks:
        me = lax.axis_index("sa")
        for number, out_ref in enumerate(refs[:2]):
            for high in range(2):
                for low in range(2):
                    mask = number * masks[0] ^ high * masks[1] ^ low * masks[2]
                    out_ref[high, low] = tiles[jnp.bitwise_xor(me, mask)]


def local_tiles(eigvecs, solutions, masks):
    _, times, eigs, _, sites = eigvecs.shape
    pairs = solutions.shape[2] * solutions.shape[3]
    columns = pairs * SPINS
    blocks = sites // LANES
    rows = COLORS * blocks * SPINS
    pitch = rows + 8 if (rows // 8) % 2 == 0 else rows
    e_view = jnp.transpose(eigvecs, (0, 1, 3, 2, 4))
    s_view = jnp.transpose(solutions, (0, 1, 2, 3, 5, 4, 6))
    s_view = s_view.reshape(2, times, pairs, COLORS, SPINS, blocks, LANES)
    s_view = jnp.swapaxes(s_view, 4, 5).reshape(2, times, pairs, rows, LANES)
    s_view = pltpu.with_memory_space_constraint(s_view, pltpu.HBM)
    vmem = pl.BlockSpec(memory_space=pltpu.VMEM)
    params = pltpu.CompilerParams(vmem_limit_bytes=VMEM_BYTES)
    split, sums = pl.pallas_call(
        split_kernel,
        out_shape=(
            jax.ShapeDtypeStruct((times, COLORS * blocks, 4 * columns, LANES), BF16),
            jax.ShapeDtypeStruct((pairs, LANES), F32),
        ),
        in_specs=[pl.BlockSpec(memory_space=pltpu.HBM)],
        out_specs=(vmem, vmem),
        scratch_shapes=[
            pltpu.VMEM((2, times, pairs, pitch, LANES), F32),
            pltpu.SemaphoreType.DMA((2, times, COLORS)),
        ],
        compiler_params=params,
        name="split",
        cost_estimate=pl.CostEstimate(
            flops=solutions.size, bytes_accessed=8 * solutions.size, transcendentals=0
        ),
    )(s_view)
    norm_row = pl.pallas_call(
        functools.partial(row_kernel, columns=columns),
        out_shape=jax.ShapeDtypeStruct((8, LANES), F32),
        in_specs=[vmem],
        out_specs=vmem,
        compiler_params=params,
        name="row",
        cost_estimate=pl.CostEstimate(flops=10**9, bytes_accessed=10**7, transcendentals=0),
    )(sums)
    tiles = jax.ShapeDtypeStruct((eigs // 8, 2 * times, 8, LANES), F32)
    block = jax.ShapeDtypeStruct((2, 2, 2 * times, 8, LANES), F32)
    make_tiles = pl.pallas_call(
        functools.partial(tile_kernel, masks=masks),
        out_shape=(block, block) if masks else tiles,
        in_specs=[vmem] * 2,
        out_specs=(vmem, vmem) if masks else vmem,
        scratch_shapes=[pltpu.VMEM(tiles.shape, F32)] if masks else [],
        compiler_params=params,
        name="tiles",
        cost_estimate=pl.CostEstimate(
            flops=24 * times * eigs * columns * COLORS * sites,
            bytes_accessed=4 * (eigvecs.size + solutions.size),
            transcendentals=0,
        ),
    )
    products = make_tiles(split, e_view)
    return products, norm_row


def finish_kernel(kept_ref, came_ref, sign_ref, out_ref):
    _, times, width = out_ref.shape
    columns = width // 8
    pairs = columns // SPINS
    row = lax.broadcasted_iota(jnp.int32, (8, LANES), 0)
    lane = lax.broadcasted_iota(jnp.int32, (8, LANES), 1)
    column = jnp.bitwise_and(lane + LANES - (row * columns) % LANES, LANES - 1)
    source = jnp.where(column < columns, (column % SPINS) * pairs + column // SPINS, 0)
    for part in range(2):
        for t in range(times):
            index = part * times + t
            tile = (kept_ref[index] + came_ref[index]) * sign_ref[t : t + 1, :]
            tile = jnp.take_along_axis(tile, source, axis=1)
            for piece in range(width // LANES):
                first = piece * LANES // columns
                edge = (first + 1) * columns - piece * LANES
                out_ref[part, t : t + 1, piece * LANES : (piece + 1) * LANES] = jnp.where(
                    lane[:1] < edge, tile[first : first + 1], tile[first + 1 : first + 2]
                )


def norm_kernel(kept_ref, extra_ref, norm_ref, *, first, cells):
    src_count, col_count = norm_ref.shape
    total = kept_ref[...] + extra_ref[...]
    for src in range(src_count):
        shift = 2 * LANES - first - src * col_count
        norm = pltpu.roll(total, shift % LANES, 1)
        norm_ref[src : src + 1, :] = norm[:1, :col_count] / cells


def swap(x, ta_mask, sa_mask):
    ta_size, sa_size = lax.axis_size("ta"), lax.axis_size("sa")
    pairs = [
        (ta * sa_size + sa, (ta ^ ta_mask) * sa_size + (sa ^ sa_mask))
        for ta in range(ta_size)
        for sa in range(sa_size)
    ]
    return lax.ppermute(x, ("ta", "sa"), pairs)


def radices_of(count):
    found = []
    for prime in (2, 3, 5, 7, 11, 13):
        while count % prime == 0:
            found.append(prime)
            count //= prime
    return found + ([count] if count > 1 else [])


def shifted(size, weight, radix, shift):
    moves = []
    for source in range(size):
        own = (source // weight) % radix
        moves.append((source, source + ((own + shift) % radix - own) * weight))
    return moves


def scatter_sum(blocks, axis):
    size = lax.axis_size(axis)
    me = lax.axis_index(axis)
    radices = radices_of(size)
    held = blocks.reshape(tuple(reversed(radices)) + blocks.shape[1:])
    weight = 1
    for depth, radix in enumerate(radices):
        dim = len(radices) - 1 - depth
        digit = (me // weight) % radix
        total = lax.dynamic_index_in_dim(held, digit, dim, False)
        for shift in range(1, radix):
            send = lax.dynamic_index_in_dim(held, (digit + shift) % radix, dim, False)
            total = total + lax.ppermute(send, axis, shifted(size, weight, radix, shift))
        held = total
        weight *= radix
    return held


def all_sum(x, axis):
    size = lax.axis_size(axis)
    weight = 1
    for radix in radices_of(size):
        total = x
        for shift in range(1, radix):
            total = total + lax.ppermute(x, axis, shifted(size, weight, radix, shift))
        x = total
        weight *= radix
    return x


def on_device(eigvecs, solutions, source_times, spin_dilution):
    _, times, eigs, _, sites = eigvecs.shape
    src_count, col_count = spin_dilution.shape
    pairs = src_count * col_count
    columns = pairs * SPINS
    devices = lax.axis_size("sa")
    cells = 12.0 * times * lax.axis_size("ta") * sites * devices
    own_width = eigs * columns // devices

    crossed = devices == 8 and lax.axis_size("ta") == 4 and eigs == 64 and columns == 96
    tiles, norm_row = local_tiles(eigvecs, solutions, MASKS if crossed else None)
    slice_times = lax.axis_index("ta") * times + jnp.arange(times, dtype=jnp.int32)
    boundary = jnp.where(slice_times[:, None] < source_times[None, :], -1.0, 1.0).astype(F32)
    chirality = jnp.where(spin_dilution < 2, 1.0, -1.0).astype(F32)
    signs = (boundary[:, :, None] * chirality[None]).reshape(times, pairs)
    if crossed:
        first = lax.broadcasted_iota(jnp.int32, (2 * times, 1, 1), 0) == 0
        norm_row = norm_row + swap(norm_row, 1, 1)
        norm_row = norm_row + swap(norm_row, 2, 1)
        kept, sent = tiles
        held = kept + swap(sent, 0, MASKS[0]) + jnp.where(first, norm_row, 0.0)
        held = held[0] + swap(held[1], 0, MASKS[1])
        kept, came = held[0], swap(held[1], 0, MASKS[2])
        line = kept[0] + came[0]
        extra = swap(line, 0, 1)
        lanes = jnp.concatenate(
            [signs] * SPINS + [jnp.ones((times, LANES - columns), F32)], 1
        )
        vmem = pl.BlockSpec(memory_space=pltpu.VMEM)
        params = pltpu.CompilerParams(vmem_limit_bytes=VMEM_BYTES)
        values = pl.pallas_call(
            finish_kernel,
            out_shape=jax.ShapeDtypeStruct((2, times, own_width), F32),
            in_specs=[vmem] * 3,
            out_specs=vmem,
            compiler_params=params,
            name="finish",
            cost_estimate=pl.CostEstimate(flops=10**7, bytes_accessed=10**6, transcendentals=0),
        )(kept, came, lanes)
        norms = pl.pallas_call(
            functools.partial(norm_kernel, first=columns, cells=cells),
            out_shape=jax.ShapeDtypeStruct((src_count, col_count), F32),
            in_specs=[vmem] * 2,
            out_specs=vmem,
            compiler_params=params,
            name="norms",
        )(line, extra)
        return values, norms
    norm_row = lax.psum(norm_row[0, columns : columns + pairs], "sa")
    values = tiles.reshape(eigs // 8, 2, times, 8, LANES)[..., :columns]
    values = values.reshape(eigs // 8, 2, times, 8, SPINS, pairs)
    values = values * signs[None, None, :, None, None]
    values = jnp.transpose(values, (1, 2, 0, 3, 5, 4)).reshape(2, times, devices, own_width)
    values = scatter_sum(jnp.transpose(values, (2, 0, 1, 3)), "sa")
    norms = all_sum(norm_row.reshape(src_count, col_count), "ta") / cells
    return values, norms


def solution(mesh):
    return jax.shard_map(
        on_device,
        mesh=mesh,
        in_specs=(
            P(None, "ta", None, None, "sa"),
            P(None, "ta", None, None, None, None, "sa"),
            P(),
            P(),
        ),
        out_specs=(P(None, "ta", "sa"), P()),
        check_vma=False,
    )
```

profile of v0, /device:TPU:0, one launch (start us, length us, event | category | flops | bytes accessed | tf_op | source)
XLA Modules:
  0.0 21.2 jit_solution(14187425129803306918)
XLA Ops:
  0.6 0.0 copy-start
  0.6 2.0 %split.1 = (bf16[2,12,384,128]{3,2,1,0:T(8,128)(2,1)S(1)}, f32[24,128]{1,0:T(8,128)S(1)}) custom-call(f32[2,2,24,48,128]{4,3,2,1,0:T(8,128)} %bitcast.27), custom_call_target="tpu_custom_call" | custom-call | flops 589824 | bytes 4718592 | tf_op jit(solution)/shard_map/split/pallas_call | solution.py:125
  2.6 0.2 %copy-done = f32[2,2,64,3,512]{4,2,3,1,0:T(8,128)S(1)} copy-done((f32[2,2,64,3,512]{4,2,3,1,0:T(8,128)S(1)}, f32[2,2,64,3,512]{4,2,3,1,0:T(8,128)}, u32[]{:S(2)}) %copy-start) | copy-done | bytes 1572888
  2.9 1.0 %tiles.1 = (f32[2,2,4,8,128]{4,3,2,1,0:T(8,128)S(1)}, f32[2,2,4,8,128]{4,3,2,1,0:T(8,128)S(1)}) custom-call(bf16[2,12,384,128]{3,2,1,0:T(8,128)(2,1)S(1)} %get-tuple-element.6.split_ref, f32[2,2,3,64,512]{4,3,2,1,0:T(8,128)S(1)} %bitcast.26), custom_call_target="tpu_custom_call" | custom-call | flops 452984832 | bytes 3932160 | tf_op jit(solution)/shard_map/tiles/pallas_call | solution.py:168
  3.8 0.0 copy-start.1
  3.8 0.0 copy-start.2
  3.9 0.6 %collective-permute-start = (f32[2,2,4,8,128]{4,3,2,1,0:T(8,128)S(1)}, f32[2,2,4,8,128]{4,3,2,1,0:T(8,128)S(1)}, u32[]{:S(2)}, u32[]{:S(2)}) collective-permute-start(f32[2,2,4,8,128]{4,3,2,1,0:T(8,128)S(1)} %get-tuple-element.8), channel_id=1, source_target_pairs={{0,1},{1,0},{2,3},{3,2},{4,5},{5,4},{6,7},{7,6},{8,9},{9,8},{10,11... | collective-permute-start | bytes 196616 | tf_op jit(solution)/shard_map/ppermute | solution.py:209
  4.4 0.1 row.1
  4.5 2.6 %collective-permute-start.1 = (f32[8,128]{1,0:T(8,128)S(1)}, f32[8,128]{1,0:T(8,128)S(1)}, u32[]{:S(2)}, u32[]{:S(2)}) collective-permute-start(f32[8,128]{1,0:T(8,128)S(1)} %row.1), channel_id=1, source_target_pairs={{0,9},{1,8},{2,11},{3,10},{4,13},{5,12},{6,15},{7,14},{8,1},{9,0},... | collective-permute-start | bytes 12296 | tf_op jit(solution)/shard_map/ppermute | solution.py:209
  7.2 0.0 copy-done.1
  7.2 1.3 %collective-permute-done.1 = f32[8,128]{1,0:T(8,128)S(1)} collective-permute-done((f32[8,128]{1,0:T(8,128)S(1)}, f32[8,128]{1,0:T(8,128)S(1)}, u32[]{:S(2)}, u32[]{:S(2)}) %collective-permute-start.1) | collective-permute-done | bytes 4128 | tf_op jit(solution)/shard_map/ppermute | solution.py:209
  8.5 1.7 %collective-permute-start.2 = (f32[8,128]{1,0:T(8,128)S(1)}, f32[8,128]{1,0:T(8,128)S(1)}, u32[]{:S(2)}, u32[]{:S(2)}) collective-permute-start(f32[8,128]{1,0:T(8,128)S(1)} %add.34), channel_id=1, source_target_pairs={{0,17},{1,16},{2,19},{3,18},{4,21},{5,20},{6,23},{7,22},{8,25},{9,... | collective-permute-start | bytes 12296 | tf_op jit(solution)/shard_map/ppermute | solution.py:209
  10.2 1.3 %collective-permute-done.2 = f32[8,128]{1,0:T(8,128)S(1)} collective-permute-done((f32[8,128]{1,0:T(8,128)S(1)}, f32[8,128]{1,0:T(8,128)S(1)}, u32[]{:S(2)}, u32[]{:S(2)}) %collective-permute-start.2) | collective-permute-done | bytes 4128 | tf_op jit(solution)/shard_map/ppermute | solution.py:209
  11.6 0.1 broadcast_select_fusion
  11.6 0.0 collective-permute-done
  11.7 1.8 %collective-permute-start.3 = (f32[2,4,8,128]{3,2,1,0:T(8,128)S(1)}, f32[2,4,8,128]{3,2,1,0:T(8,128)S(1)}, u32[]{:S(2)}, u32[]{:S(2)}) collective-permute-start(f32[2,4,8,128]{3,2,1,0:T(8,128)S(1)} %slice_bitcast_fusion), channel_id=1, source_target_pairs={{0,3},{1,2},{2,1},{3,0},{4,7},{5,6},{6,5},{7,4},{8,11},{9,10},{10,... | collective-permute-start | bytes 98312 | tf_op jit(solution)/shard_map/ppermute | solution.py:209
  13.5 1.7 %collective-permute-done.3 = f32[2,4,8,128]{3,2,1,0:T(8,128)S(1)} collective-permute-done((f32[2,4,8,128]{3,2,1,0:T(8,128)S(1)}, f32[2,4,8,128]{3,2,1,0:T(8,128)S(1)}, u32[]{:S(2)}, u32[]{:S(2)}) %collective-permute-start.3) | collective-permute-done | bytes 32800 | tf_op jit(solution)/shard_map/ppermute | solution.py:209
  15.2 2.7 %collective-permute-start.4 = (f32[4,8,128]{2,1,0:T(8,128)S(1)}, f32[4,8,128]{2,1,0:T(8,128)S(1)}, u32[]{:S(2)}, u32[]{:S(2)}) collective-permute-start(f32[4,8,128]{2,1,0:T(8,128)S(1)} %get-tuple-element.10), channel_id=1, source_target_pairs={{0,5},{1,4},{2,7},{3,6},{4,1},{5,0},{6,3},{7,2},{8,13},{9,12},{10,... | collective-permute-start | bytes 49160 | tf_op jit(solution)/shard_map/ppermute | solution.py:209
  17.9 0.0 copy-done.2
  17.9 0.1 compare_select_fusion.1
  18.0 0.1 mul.22
  18.1 0.1 mul.23
  18.2 0.1 mul.24
  18.2 1.1 %collective-permute-done.4.came_ref = f32[4,8,128]{2,1,0:T(8,128)S(1)} collective-permute-done((f32[4,8,128]{2,1,0:T(8,128)S(1)}, f32[4,8,128]{2,1,0:T(8,128)S(1)}, u32[]{:S(2)}, u32[]{:S(2)}) %collective-permute-start.4) | collective-permute-done | bytes 16416 | tf_op jit(solution)/shard_map/ppermute | solution.py:209
  19.4 0.1 collective-permute-start.5
  19.5 0.1 concatenate.3.sign_ref
  19.6 0.7 %finish.1 = f32[2,2,768]{2,1,0:T(2,128)} custom-call(f32[4,8,128]{2,1,0:T(8,128)S(1)} %get-tuple-element.11.kept_ref, f32[4,8,128]{2,1,0:T(8,128)S(1)} %collective-permute-done.4.came_ref, f32[2,128]{1,0:T(2,128)S(1)} %concatenate.3.sign_ref), custom_call_target="tpu_custom_call" | custom-call | flops 10000000 | bytes 1000000 | tf_op jit(solution)/shard_map/finish/pallas_call | solution.py:289
  20.3 0.3 %collective-permute-done.5.extra_ref = f32[8,128]{1,0:T(8,128)S(1)} collective-permute-done((f32[8,128]{1,0:T(8,128)S(1)}, f32[8,128]{1,0:T(8,128)S(1)}, u32[]{:S(2)}, u32[]{:S(2)}) %collective-permute-start.5) | collective-permute-done | bytes 4128 | tf_op jit(solution)/shard_map/ppermute | solution.py:209
  20.5 0.7 %norms.1 = f32[3,8]{1,0:T(4,128)} custom-call(f32[8,128]{1,0:T(8,128)S(1)} %fusion.1.kept_ref, f32[8,128]{1,0:T(8,128)S(1)} %collective-permute-done.5.extra_ref), custom_call_target="tpu_custom_call" | custom-call | tf_op jit(solution)/shard_map/norms/pallas_call | solution.py:298
  (12 shorter events, 0.1 us)
Async XLA Ops:
  0.6 2.2 %copy-start = (f32[2,2,64,3,512]{4,2,3,1,0:T(8,128)S(1)}, f32[2,2,64,3,512]{4,2,3,1,0:T(8,128)}, u32[]{:S(2)}) copy-start(f32[2,2,64,3,512]{4,2,3,1,0:T(8,128)} %param.4) | copy-start | bytes 4718596
  3.8 3.3 %copy-start.1 = (s32[3,8]{1,0:T(4,128)S(1)}, s32[3,8]{1,0:T(4,128)}, u32[]{:S(2)}) copy-start(s32[3,8]{1,0:T(4,128)} %param.7) | copy-start | bytes 292
  3.8 14.1 %copy-start.2 = (s32[3]{0:T(128)S(1)}, s32[3]{0:T(128)}, u32[]{:S(2)}) copy-start(s32[3]{0:T(128)} %param.6) | copy-start | bytes 40
  3.9 7.8 %collective-permute-start = (f32[2,2,4,8,128]{4,3,2,1,0:T(8,128)S(1)}, f32[2,2,4,8,128]{4,3,2,1,0:T(8,128)S(1)}, u32[]{:S(2)}, u32[]{:S(2)}) collective-permute-start(f32[2,2,4,8,128]{4,3,2,1,0:T(8,128)S(1)} %get-tuple-element.8), channel_id=1, source_target_pairs={{0,1},{1,0},{2,3},{3,2},{4,5},{5,4},{6,7},{7,6},{8,9},{9,8},{10,11... | collective-permute-start | bytes 196616 | tf_op jit(solution)/shard_map/ppermute | solution.py:209
  4.5 3.9 %collective-permute-start.1 = (f32[8,128]{1,0:T(8,128)S(1)}, f32[8,128]{1,0:T(8,128)S(1)}, u32[]{:S(2)}, u32[]{:S(2)}) collective-permute-start(f32[8,128]{1,0:T(8,128)S(1)} %row.1), channel_id=1, source_target_pairs={{0,9},{1,8},{2,11},{3,10},{4,13},{5,12},{6,15},{7,14},{8,1},{9,0},... | collective-permute-start | bytes 12296 | tf_op jit(solution)/shard_map/ppermute | solution.py:209
  8.5 3.1 %collective-permute-start.2 = (f32[8,128]{1,0:T(8,128)S(1)}, f32[8,128]{1,0:T(8,128)S(1)}, u32[]{:S(2)}, u32[]{:S(2)}) collective-permute-start(f32[8,128]{1,0:T(8,128)S(1)} %add.34), channel_id=1, source_target_pairs={{0,17},{1,16},{2,19},{3,18},{4,21},{5,20},{6,23},{7,22},{8,25},{9,... | collective-permute-start | bytes 12296 | tf_op jit(solution)/shard_map/ppermute | solution.py:209
  11.7 3.5 %collective-permute-start.3 = (f32[2,4,8,128]{3,2,1,0:T(8,128)S(1)}, f32[2,4,8,128]{3,2,1,0:T(8,128)S(1)}, u32[]{:S(2)}, u32[]{:S(2)}) collective-permute-start(f32[2,4,8,128]{3,2,1,0:T(8,128)S(1)} %slice_bitcast_fusion), channel_id=1, source_target_pairs={{0,3},{1,2},{2,1},{3,0},{4,7},{5,6},{6,5},{7,4},{8,11},{9,10},{10,... | collective-permute-start | bytes 98312 | tf_op jit(solution)/shard_map/ppermute | solution.py:209
  15.2 4.2 %collective-permute-start.4 = (f32[4,8,128]{2,1,0:T(8,128)S(1)}, f32[4,8,128]{2,1,0:T(8,128)S(1)}, u32[]{:S(2)}, u32[]{:S(2)}) collective-permute-start(f32[4,8,128]{2,1,0:T(8,128)S(1)} %get-tuple-element.10), channel_id=1, source_target_pairs={{0,5},{1,4},{2,7},{3,6},{4,1},{5,0},{6,3},{7,2},{8,13},{9,12},{10,... | collective-permute-start | bytes 49160 | tf_op jit(solution)/shard_map/ppermute | solution.py:209
  19.4 1.2 %collective-permute-start.5 = (f32[8,128]{1,0:T(8,128)S(1)}, f32[8,128]{1,0:T(8,128)S(1)}, u32[]{:S(2)}, u32[]{:S(2)}) collective-permute-start(f32[8,128]{1,0:T(8,128)S(1)} %fusion.1.kept_ref), channel_id=1, source_target_pairs={{0,1},{1,0},{2,3},{3,2},{4,5},{5,4},{6,7},{7,6},{8,9},{9,8},{10,11... | collective-permute-start | bytes 12296 | tf_op jit(solution)/shard_map/ppermute | solution.py:209
where the time goes:
time: 21.3 us; the launch traced here: 21.2 us
  starting transfers between devices  9.55 us (45%)
  waiting for transfers between devices  5.73 us (27%)
  Pallas kernels  4.41 us (21%)
  between operations  0.7 us (3%)
  local copies, waits for them, and re-layouts  0.61 us (3%)
    ppermute x6, starting transfers between devices, swap(): return lax.ppermute(x, ('ta', 'sa'), pairs)  9.55 us
    ppermute x6, waiting for transfers between devices, swap(): return lax.ppermute(x, ('ta', 'sa'), pairs)  5.73 us
    pallas_call x1, Pallas kernels, local_tiles(): pl.pallas_call(split_kernel, out_shape=(jax.ShapeDtypeStruct((times, COLO...  1.97 us
    pallas_call x1, Pallas kernels, local_tiles(): products = make_tiles(split, e_view)  0.96 us
    pallas_call x1, Pallas kernels, on_device(): pl.pallas_call(finish_kernel, out_shape=jax.ShapeDtypeStruct((2, times, o...  0.7 us
    pallas_call x1, Pallas kernels, on_device(): pl.pallas_call(functools.partial(norm_kernel, first=columns, cells=cells)...  0.65 us
  transfers between devices with their start and end apart: 6, of which 5 were waited for; matrix products, arithmetic and copies ran while one was open for 2% of the time, Pallas kernels for 4%

commit v1 on v0

--- a/solution.py
+++ b/solution.py
@@ -273,8 +273,9 @@
     signs = (boundary[:, :, None] * chirality[None]).reshape(times, pairs)
     if crossed:
         first = lax.broadcasted_iota(jnp.int32, (2 * times, 1, 1), 0) == 0
-        norm_row = norm_row + swap(norm_row, 1, 1)
-        norm_row = norm_row + swap(norm_row, 2, 1)
+        own = norm_row
+        for ta_mask in (3, 1, 2):
+            norm_row = norm_row + swap(own, ta_mask, 1)
         kept, sent = tiles
         held = kept + swap(sent, 0, MASKS[0]) + jnp.where(first, norm_row, 0.0)
         held = held[0] + swap(held[1], 0, MASKS[1])

time: 21.3 us -> 20.5 us (0.962)
  starting transfers between devices: 9.55 us -> 8.19 us
  waiting for transfers between devices: 5.73 us -> 6.6 us
  local copies, waits for them, and re-layouts: 0.61 us -> 0.36 us
    ppermute x6 -> x7, starting transfers between devices: 9.55 us -> 8.19 us  [swap(): return lax.ppermute(x, ('ta', 'sa'), pairs)]
    ppermute x6 -> x7, waiting for transfers between devices: 5.73 us -> 6.6 us  [swap(): return lax.ppermute(x, ('ta', 'sa'), pairs)]
    unnamed x6, local copies, waits for them, and re-layouts: 0.26 us -> 0.01 us
  transfers between devices with their start and end apart: 6 -> 7, of which waited for: 5 -> 5; matrix products, arithmetic and copies ran while one was open for 2% -> 2% of each run, Pallas kernels for 4% -> 8%
where the time goes in v1:
time: 20.5 us; the launch traced here: 20.4 us
  starting transfers between devices  8.19 us (40%)
  waiting for transfers between devices  6.6 us (32%)
  Pallas kernels  4.31 us (21%)
  between operations  0.72 us (4%)
  local copies, waits for them, and re-layouts  0.36 us (2%)
    ppermute x7, starting transfers between devices, swap(): return lax.ppermute(x, ('ta', 'sa'), pairs)  8.19 us
    ppermute x7, waiting for transfers between devices, swap(): return lax.ppermute(x, ('ta', 'sa'), pairs)  6.6 us
    pallas_call x1, Pallas kernels, local_tiles(): pl.pallas_call(split_kernel, out_shape=(jax.ShapeDtypeStruct((times, COLO...  1.87 us
    pallas_call x1, Pallas kernels, local_tiles(): products = make_tiles(split, e_view)  0.96 us
    pallas_call x1, Pallas kernels, on_device(): pl.pallas_call(finish_kernel, out_shape=jax.ShapeDtypeStruct((2, times, o...  0.7 us
    pallas_call x1, Pallas kernels, on_device(): pl.pallas_call(functools.partial(norm_kernel, first=columns, cells=cells)...  0.65 us
  transfers between devices with their start and end apart: 7, of which 5 were waited for; matrix products, arithmetic and copies ran while one was open for 2% of the time, Pallas kernels for 8%

profile of v1, /device:TPU:0, one launch (start us, length us, event | category | flops | bytes accessed | tf_op | source)
XLA Modules:
  0.0 20.4 jit_solution(4104145095164475430)
XLA Ops:
  0.6 1.9 %split.1 = (bf16[2,12,384,128]{3,2,1,0:T(8,128)(2,1)S(1)}, f32[24,128]{1,0:T(8,128)S(1)}) custom-call(f32[2,2,24,48,128]{4,3,2,1,0:T(8,128)} %bitcast.27), custom_call_target="tpu_custom_call" | custom-call | flops 589824 | bytes 4718592 | tf_op jit(solution)/shard_map/split/pallas_call | solution.py:125
  2.5 0.0 copy-start
  2.5 0.1 row.1
  2.6 0.0 copy-start.1
  2.6 0.0 copy-start.2
  2.6 2.5 %collective-permute-start.3 = (f32[8,128]{1,0:T(8,128)S(1)}, f32[8,128]{1,0:T(8,128)S(1)}, u32[]{:S(2)}, u32[]{:S(2)}) collective-permute-start(f32[8,128]{1,0:T(8,128)S(1)} %row.1), channel_id=1, source_target_pairs={{0,17},{1,16},{2,19},{3,18},{4,21},{5,20},{6,23},{7,22},{8,25},{9,... | collective-permute-start | bytes 12296 | tf_op jit(solution)/shard_map/ppermute | solution.py:209
  5.1 1.8 %collective-permute-start.2 = (f32[8,128]{1,0:T(8,128)S(1)}, f32[8,128]{1,0:T(8,128)S(1)}, u32[]{:S(2)}, u32[]{:S(2)}) collective-permute-start(f32[8,128]{1,0:T(8,128)S(1)} %row.1), channel_id=1, source_target_pairs={{0,9},{1,8},{2,11},{3,10},{4,13},{5,12},{6,15},{7,14},{8,1},{9,0},... | collective-permute-start | bytes 12296 | tf_op jit(solution)/shard_map/ppermute | solution.py:209
  6.9 0.0 collective-permute-start.1
  6.9 0.0 copy-done
  6.9 1.0 %tiles.1 = (f32[2,2,4,8,128]{4,3,2,1,0:T(8,128)S(1)}, f32[2,2,4,8,128]{4,3,2,1,0:T(8,128)S(1)}) custom-call(bf16[2,12,384,128]{3,2,1,0:T(8,128)(2,1)S(1)} %get-tuple-element.6.split_ref, f32[2,2,3,64,512]{4,3,2,1,0:T(8,128)S(1)} %bitcast.26), custom_call_target="tpu_custom_call" | custom-call | flops 452984832 | bytes 3932160 | tf_op jit(solution)/shard_map/tiles/pallas_call | solution.py:168
  7.9 0.1 collective-permute-start
  8.0 0.0 copy-done.1
  8.0 0.0 collective-permute-done.3
  8.0 0.2 collective-permute-done.2
  8.2 2.6 %collective-permute-done.1 = f32[8,128]{1,0:T(8,128)S(1)} collective-permute-done((f32[8,128]{1,0:T(8,128)S(1)}, f32[8,128]{1,0:T(8,128)S(1)}, u32[]{:S(2)}, u32[]{:S(2)}) %collective-permute-start.1) | collective-permute-done | bytes 4128 | tf_op jit(solution)/shard_map/ppermute | solution.py:209
  10.8 0.1 broadcast_select_fusion
  10.9 0.0 collective-permute-done
  11.0 1.4 %collective-permute-start.4 = (f32[2,4,8,128]{3,2,1,0:T(8,128)S(1)}, f32[2,4,8,128]{3,2,1,0:T(8,128)S(1)}, u32[]{:S(2)}, u32[]{:S(2)}) collective-permute-start(f32[2,4,8,128]{3,2,1,0:T(8,128)S(1)} %slice_bitcast_fusion), channel_id=1, source_target_pairs={{0,3},{1,2},{2,1},{3,0},{4,7},{5,6},{6,5},{7,4},{8,11},{9,10},{10,... | collective-permute-start | bytes 98312 | tf_op jit(solution)/shard_map/ppermute | solution.py:209
  12.3 2.1 %collective-permute-done.4 = f32[2,4,8,128]{3,2,1,0:T(8,128)S(1)} collective-permute-done((f32[2,4,8,128]{3,2,1,0:T(8,128)S(1)}, f32[2,4,8,128]{3,2,1,0:T(8,128)S(1)}, u32[]{:S(2)}, u32[]{:S(2)}) %collective-permute-start.4) | collective-permute-done | bytes 32800 | tf_op jit(solution)/shard_map/ppermute | solution.py:209
  14.4 2.4 %collective-permute-start.5 = (f32[4,8,128]{2,1,0:T(8,128)S(1)}, f32[4,8,128]{2,1,0:T(8,128)S(1)}, u32[]{:S(2)}, u32[]{:S(2)}) collective-permute-start(f32[4,8,128]{2,1,0:T(8,128)S(1)} %get-tuple-element.10), channel_id=1, source_target_pairs={{0,5},{1,4},{2,7},{3,6},{4,1},{5,0},{6,3},{7,2},{8,13},{9,12},{10,... | collective-permute-start | bytes 49160 | tf_op jit(solution)/shard_map/ppermute | solution.py:209
  16.8 0.0 copy-done.2
  16.8 0.1 compare_select_fusion.1
  16.9 0.1 mul.22
  17.0 0.1 mul.23
  17.0 0.1 mul.24
  17.1 1.4 %collective-permute-done.5.came_ref = f32[4,8,128]{2,1,0:T(8,128)S(1)} collective-permute-done((f32[4,8,128]{2,1,0:T(8,128)S(1)}, f32[4,8,128]{2,1,0:T(8,128)S(1)}, u32[]{:S(2)}, u32[]{:S(2)}) %collective-permute-start.5) | collective-permute-done | bytes 16416 | tf_op jit(solution)/shard_map/ppermute | solution.py:209
  18.6 0.1 collective-permute-start.6
  18.7 0.1 concatenate.3.sign_ref
  18.8 0.7 %finish.1 = f32[2,2,768]{2,1,0:T(2,128)} custom-call(f32[4,8,128]{2,1,0:T(8,128)S(1)} %get-tuple-element.11.kept_ref, f32[4,8,128]{2,1,0:T(8,128)S(1)} %collective-permute-done.5.came_ref, f32[2,128]{1,0:T(2,128)S(1)} %concatenate.3.sign_ref), custom_call_target="tpu_custom_call" | custom-call | flops 10000000 | bytes 1000000 | tf_op jit(solution)/shard_map/finish/pallas_call | solution.py:290
  19.5 0.2 %collective-permute-done.6.extra_ref = f32[8,128]{1,0:T(8,128)S(1)} collective-permute-done((f32[8,128]{1,0:T(8,128)S(1)}, f32[8,128]{1,0:T(8,128)S(1)}, u32[]{:S(2)}, u32[]{:S(2)}) %collective-permute-start.6) | collective-permute-done | bytes 4128 | tf_op jit(solution)/shard_map/ppermute | solution.py:209
  19.7 0.7 %norms.1 = f32[3,8]{1,0:T(4,128)} custom-call(f32[8,128]{1,0:T(8,128)S(1)} %fusion.1.kept_ref, f32[8,128]{1,0:T(8,128)S(1)} %collective-permute-done.6.extra_ref), custom_call_target="tpu_custom_call" | custom-call | tf_op jit(solution)/shard_map/norms/pallas_call | solution.py:299
  (11 shorter events, 0.1 us)
Async XLA Ops:
  2.5 4.4 %copy-start = (f32[2,2,64,3,512]{4,2,3,1,0:T(8,128)S(1)}, f32[2,2,64,3,512]{4,2,3,1,0:T(8,128)}, u32[]{:S(2)}) copy-start(f32[2,2,64,3,512]{4,2,3,1,0:T(8,128)} %param.4) | copy-start | bytes 4718596
  2.6 5.3 %copy-start.1 = (s32[3,8]{1,0:T(4,128)S(1)}, s32[3,8]{1,0:T(4,128)}, u32[]{:S(2)}) copy-start(s32[3,8]{1,0:T(4,128)} %param.7) | copy-start | bytes 292
  2.6 14.2 %copy-start.2 = (s32[3]{0:T(128)S(1)}, s32[3]{0:T(128)}, u32[]{:S(2)}) copy-start(s32[3]{0:T(128)} %param.6) | copy-start | bytes 40
  2.6 5.4 %collective-permute-start.3 = (f32[8,128]{1,0:T(8,128)S(1)}, f32[8,128]{1,0:T(8,128)S(1)}, u32[]{:S(2)}, u32[]{:S(2)}) collective-permute-start(f32[8,128]{1,0:T(8,128)S(1)} %row.1), channel_id=1, source_target_pairs={{0,17},{1,16},{2,19},{3,18},{4,21},{5,20},{6,23},{7,22},{8,25},{9,... | collective-permute-start | bytes 12296 | tf_op jit(solution)/shard_map/ppermute | solution.py:209
  5.1 3.1 %collective-permute-start.2 = (f32[8,128]{1,0:T(8,128)S(1)}, f32[8,128]{1,0:T(8,128)S(1)}, u32[]{:S(2)}, u32[]{:S(2)}) collective-permute-start(f32[8,128]{1,0:T(8,128)S(1)} %row.1), channel_id=1, source_target_pairs={{0,9},{1,8},{2,11},{3,10},{4,13},{5,12},{6,15},{7,14},{8,1},{9,0},... | collective-permute-start | bytes 12296 | tf_op jit(solution)/shard_map/ppermute | solution.py:209
  6.9 4.0 %collective-permute-start.1 = (f32[8,128]{1,0:T(8,128)S(1)}, f32[8,128]{1,0:T(8,128)S(1)}, u32[]{:S(2)}, u32[]{:S(2)}) collective-permute-start(f32[8,128]{1,0:T(8,128)S(1)} %row.1), channel_id=1, source_target_pairs={{0,25},{1,24},{2,27},{3,26},{4,29},{5,28},{6,31},{7,30},{8,17},{9,... | collective-permute-start | bytes 12296 | tf_op jit(solution)/shard_map/ppermute | solution.py:209
  7.9 3.0 %collective-permute-start = (f32[2,2,4,8,128]{4,3,2,1,0:T(8,128)S(1)}, f32[2,2,4,8,128]{4,3,2,1,0:T(8,128)S(1)}, u32[]{:S(2)}, u32[]{:S(2)}) collective-permute-start(f32[2,2,4,8,128]{4,3,2,1,0:T(8,128)S(1)} %get-tuple-element.8), channel_id=1, source_target_pairs={{0,1},{1,0},{2,3},{3,2},{4,5},{5,4},{6,7},{7,6},{8,9},{9,8},{10,11... | collective-permute-start | bytes 196616 | tf_op jit(solution)/shard_map/ppermute | solution.py:209
  11.0 3.5 %collective-permute-start.4 = (f32[2,4,8,128]{3,2,1,0:T(8,128)S(1)}, f32[2,4,8,128]{3,2,1,0:T(8,128)S(1)}, u32[]{:S(2)}, u32[]{:S(2)}) collective-permute-start(f32[2,4,8,128]{3,2,1,0:T(8,128)S(1)} %slice_bitcast_fusion), channel_id=1, source_target_pairs={{0,3},{1,2},{2,1},{3,0},{4,7},{5,6},{6,5},{7,4},{8,11},{9,10},{10,... | collective-permute-start | bytes 98312 | tf_op jit(solution)/shard_map/ppermute | solution.py:209
  14.4 4.1 %collective-permute-start.5 = (f32[4,8,128]{2,1,0:T(8,128)S(1)}, f32[4,8,128]{2,1,0:T(8,128)S(1)}, u32[]{:S(2)}, u32[]{:S(2)}) collective-permute-start(f32[4,8,128]{2,1,0:T(8,128)S(1)} %get-tuple-element.10), channel_id=1, source_target_pairs={{0,5},{1,4},{2,7},{3,6},{4,1},{5,0},{6,3},{7,2},{8,13},{9,12},{10,... | collective-permute-start | bytes 49160 | tf_op jit(solution)/shard_map/ppermute | solution.py:209
  18.6 1.2 %collective-permute-start.6 = (f32[8,128]{1,0:T(8,128)S(1)}, f32[8,128]{1,0:T(8,128)S(1)}, u32[]{:S(2)}, u32[]{:S(2)}) collective-permute-start(f32[8,128]{1,0:T(8,128)S(1)} %fusion.1.kept_ref), channel_id=1, source_target_pairs={{0,1},{1,0},{2,3},{3,2},{4,5},{5,4},{6,7},{7,6},{8,9},{9,8},{10,11... | collective-permute-start | bytes 12296 | tf_op jit(solution)/shard_map/ppermute | solution.py:209
